TPU v7x, 32 devices: a whole 2x2x4 slice. The times are simulated.
32 devices in a mesh: row: 8 (over y, x, core), col: 4 (over z).
Axes of the slice: x: 2, y: 2, z: 4, core: 2. Of those that a mesh axis runs over, the one named last changes fastest.
Arguments:
- velocity: float32 [128, 128, 2048], P(None, 'row', 'col'), may hold values from -6 to 6
- symbol_x: float32 [128], replicated, may hold values from 0.3 to 3
- symbol_y: float32 [128], replicated, may hold values from 0.3 to 3
- symbol_z: float32 [2048], replicated, may hold values from 0.3 to 3
Outputs:
- coefficients: float32 [128, 128, 2048], P('row', 'col')
All inputs are finite; a program needn't handle non-finite values.
Results may differ from a plain program's by a relative error of at most 0.000076.
Values sent between devices are 32-bit elements; how exact they have to be, the bound alone decides.
A program may use at most 192 MiB of HBM per device.

v0:
```python
import jax
import jax.numpy as jnp
from jax import lax
from jax.sharding import PartitionSpec as P


def mode_table(count):
    rank = jnp.arange(count)
    angle = 2.0 * jnp.pi / count * (rank[:, None] * rank[None, :] % count).astype(jnp.float32)
    return (jnp.cos(angle) + jnp.sin(angle)) * count ** (-0.5)


def along_dim(values, dim):
    moved = jnp.tensordot(
        values, mode_table(values.shape[dim]), axes=([dim], [0]), precision=lax.Precision.HIGHEST
    )
    return jnp.moveaxis(moved, -1, dim)


def local(velocity, symbol_x, symbol_y, symbol_z):
    part_values = velocity
    part_values = along_dim(part_values, 0)
    part_values = lax.all_to_all(part_values, "row", split_axis=0, concat_axis=1, tiled=True)
    part_values = along_dim(part_values, 1)
    pencil_values = part_values
    pencil_values = lax.all_to_all(pencil_values, "col", split_axis=1, concat_axis=2, tiled=True)
    pencil_values = along_dim(pencil_values, 2)
    share_x = pencil_values.shape[0]
    part_x = lax.dynamic_slice_in_dim(symbol_x, lax.axis_index("row") * share_x, share_x)
    share_y = pencil_values.shape[1]
    part_y = lax.dynamic_slice_in_dim(symbol_y, lax.axis_index("col") * share_y, share_y)
    symbol = part_x[:, None, None] + part_y[None, :, None] + symbol_z[None, None, :]
    pencil_values = pencil_values * ((1.0 - 0.2 * symbol) / (1.0 + 0.2 * symbol))
    return pencil_values


def solution(mesh):
    placed = (P(None, "row", "col"), P(), P(), P())
    return jax.shard_map(
        local, mesh=mesh, in_specs=placed, out_specs=P("row", "col", None), check_vma=False
    )
```

profile of v0, /device:TPU:1, one launch (start us, length us, event | category | flops | bytes accessed | tf_op | source)
XLA Modules:
  0.0 223.5 jit_solution(18273751174371291723)
XLA Ops:
  0.0 9.0 %fusion.19 = f32[128,16,512]{2,0,1:T(8,128)S(1)} fusion(f32[128,16,512]{2,1,0:T(8,128)} %param.4), kind=kOutput, calls=%fused_computation.20 | convolution fusion | flops 1610874880 | bytes 8388608 | tf_op jit(solution)/shard_map/dot_general | solution.py:14
  9.0 2.4 %copy.24 = f32[128,16,512]{2,1,0:T(8,128)S(1)} copy(f32[128,16,512]{2,0,1:T(8,128)S(1)} %fusion.19) | data formatting | bytes 8388608 | tf_op jit(solution)/shard_map/dot_general | solution.py:14
  11.5 52.8 %all_to_all.36 = f32[128,16,512]{2,1,0:T(8,128)S(1)} all-to-all(f32[128,16,512]{2,1,0:T(8,128)S(1)} %copy.24), channel_id=1, replica_groups=mesh['row'=8,'col'=4] {'row'}, dimensions={0} | all-to-all | bytes 8388608 | tf_op jit(solution)/shard_map/all_to_all | solution.py:23
  64.3 0.8 copy.25
  65.1 8.6 %convolution_bitcast_fusion = f32[16,128,512]{1,2,0:T(8,128)} fusion(f32[16,128,512]{2,1,0:T(8,128)S(1)} %bitcast.28), kind=kOutput, calls=%fused_computation.23 | convolution fusion | flops 1610874880 | bytes 8388608 | tf_op jit(solution)/shard_map/dot_general | solution.py:14
  73.7 5.5 %copy.27 = f32[16,128,512]{2,0,1:T(8,128)} copy(f32[16,128,512]{1,2,0:T(8,128)} %convolution_bitcast_fusion) | data formatting | bytes 8388608 | tf_op jit(solution)/shard_map/transpose | solution.py:17
  79.2 0.0 copy-start.1
  79.3 0.0 copy-start.2
  79.3 5.1 %all-to-all-start.1 = ((f32[16,128,512]{2,0,1:T(8,128)}), f32[16,128,512]{2,0,1:T(8,128)}, u32[]{:S(2)}, u32[]{:S(2)}) async-start(f32[16,128,512]{2,0,1:T(8,128)} %copy.27), calls=%async_computation.1 | async-start | bytes 8388608 | tf_op jit(solution)/shard_map/all_to_all | solution.py:26
  84.4 0.0 copy-done.1
  84.4 0.1 dynamic_slice.7
  84.5 0.0 copy-done.2
  84.5 0.1 dynamic_slice.6
  84.6 0.1 broadcast_add_fusion
  84.7 67.7 %fusion.51 = f32[2048,2048,1]{1,0,2:T(8,128)} fusion(), kind=kLoop, calls=%fused_computation.7.clone.clone.clone.1 | loop fusion | flops 67108864 | bytes 16777216 | tf_op jit(solution)/shard_map/dot_general | solution.py:14
  152.3 24.7 %all-to-all-done.1 = f32[16,128,512]{2,0,1:T(8,128)} async-done(((f32[16,128,512]{2,0,1:T(8,128)}), f32[16,128,512]{2,0,1:T(8,128)}, u32[]{:S(2)}, u32[]{:S(2)}) %all-to-all-start.1) | async-done | bytes 4194336 | tf_op jit(solution)/shard_map/all_to_all | solution.py:26
  177.1 6.9 %copy.29 = f32[16,32,4,512]{3,2,1,0:T(4,128)} copy(f32[16,32,4,512]{3,0,1,2:T(8,128)} %bitcast.8) | data formatting | bytes 8388608 | tf_op jit(solution)/shard_map/all_to_all | solution.py:26
  184.0 0.0 copy-start
  184.0 6.1 %all_to_all.33 = f32[16,32,2048]{2,1,0:T(8,128)} reshape(f32[16,32,4,512]{3,2,1,0:T(4,128)} %copy.29) | data formatting | bytes 8388608 | tf_op jit(solution)/shard_map/all_to_all | solution.py:26
  190.0 0.0 copy-done
  190.0 33.4 %divide_multiply_fusion = f32[16,32,2048]{2,1,0:T(8,128)} fusion(f32[16,32,2048]{2,1,0:T(8,128)} %all_to_all.33, f32[2048]{0:T(1024)S(1)} %copy-done, f32[16,32]{1,0:T(8,128)S(1)} %broadcast_add_fusion, f32[2048,2048,1]{1,0,2:T(8,128)} %fusion.51), kind=kOutput, calls=%fused_computation.22 | convolution fusion | flops 25776095232 | bytes 25176064 | tf_op jit(solution)/shard_map/dot_general | solution.py:14
Async XLA Ops:
  79.2 5.2 %copy-start.1 = (f32[128]{0:T(128)S(1)}, f32[128]{0:T(128)}, u32[]{:S(2)}) copy-start(f32[128]{0:T(128)} %param.6) | copy-start | bytes 1540
  79.3 5.3 %copy-start.2 = (f32[128]{0:T(128)S(1)}, f32[128]{0:T(128)}, u32[]{:S(2)}) copy-start(f32[128]{0:T(128)} %param.5) | copy-start | bytes 1540
  79.3 97.8 %all-to-all-start.1 = ((f32[16,128,512]{2,0,1:T(8,128)}), f32[16,128,512]{2,0,1:T(8,128)}, u32[]{:S(2)}, u32[]{:S(2)}) async-start(f32[16,128,512]{2,0,1:T(8,128)} %copy.27), calls=%async_computation.1 | async-start | bytes 8388608 | tf_op jit(solution)/shard_map/all_to_all | solution.py:26
  184.0 6.1 %copy-start = (f32[2048]{0:T(1024)S(1)}, f32[2048]{0:T(1024)}, u32[]{:S(2)}) copy-start(f32[2048]{0:T(1024)} %param.7) | copy-start | bytes 24580
where the time goes:
time: 225 us; the launch traced here: 223 us
  other arithmetic  67.8 us (30%)
  blocking collectives  52.8 us (23%)
  matrix products  51 us (23%)
  waiting for transfers between devices  24.7 us (11%)
  local copies, waits for them, and re-layouts  21.9 us (10%)
  starting transfers between devices  5.15 us (2%)
    dot_general x1, other arithmetic, along_dim(): jnp.tensordot(values, mode_table(values.shape[dim]), axes=([dim], [0]), p...  67.7 us
    all_to_all x1, blocking collectives, local(): lax.all_to_all(part_values, 'row', split_axis=0, concat_axis=1, tiled=True)  52.8 us
    dot_general x3, matrix products, along_dim(): jnp.tensordot(values, mode_table(values.shape[dim]), axes=([dim], [0]), p...  51 us
    all_to_all x1, waiting for transfers between devices, local(): lax.all_to_all(pencil_values, 'col', split_axis=1, concat_axis=2, tiled=T...  24.7 us
    all_to_all x2, local copies, waits for them, and re-layouts, local(): lax.all_to_all(pencil_values, 'col', split_axis=1, concat_axis=2, tiled=T...  13 us
    transpose x1, local copies, waits for them, and re-layouts, along_dim(): return jnp.moveaxis(moved, -1, dim)  5.51 us
    all_to_all x1, starting transfers between devices, local(): lax.all_to_all(pencil_values, 'col', split_axis=1, concat_axis=2, tiled=T...  5.15 us
  transfers between devices with their start and end apart: 1, of which 1 were waited for; matrix products, arithmetic and copies ran while one was open for 30% of the time, Pallas kernels for 0%

commit v1 on v0

v1 whole, which is shorter than its diff:
```python
import functools

import jax
import jax.numpy as jnp
import numpy as np
from jax import lax
from jax.experimental import pallas as pl
from jax.experimental.pallas import tpu as pltpu
from jax.sharding import PartitionSpec as P

SUB = 8
MESH = pl.DeviceIdType.MESH


def mode_table(count):
    rank = jnp.arange(count)
    angle = 2.0 * jnp.pi / count * (rank[:, None] * rank[None, :] % count).astype(jnp.float32)
    return (jnp.cos(angle) + jnp.sin(angle)) * count ** (-0.5)


def along_dim(values, dim):
    moved = jnp.tensordot(
        values, mode_table(values.shape[dim]), axes=([dim], [0]), precision=lax.Precision.HIGHEST
    )
    return jnp.moveaxis(moved, -1, dim)


def fixed_table(count):
    rank = np.arange(count)
    angle = 2.0 * np.pi / count * (rank[:, None] * rank[None, :] % count)
    return ((np.cos(angle) + np.sin(angle)) * count ** (-0.5)).astype(np.float32)


def halves(table):
    high = table.astype(jnp.bfloat16)
    low = (table - high.astype(np.float32)).astype(jnp.bfloat16)
    return high, low


def split(values):
    high = values.astype(jnp.bfloat16)
    low = (values - high.astype(jnp.float32)).astype(jnp.bfloat16)
    return high, low


def product(a, b):
    return jnp.dot(a, b, preferred_element_type=jnp.float32)


def flipped(index, mask):
    out = index
    bit = 1
    while bit <= mask:
        if mask & bit:
            out = out + bit * (1 - 2 * ((index // bit) % 2))
        bit *= 2
    return out


def kernel(
    dims, v_hbm, w_hbm, h_ref, t_hbm, out_ref,
    v, w, t, v_parts, xs, rbuf, ybuf, zbuf, lhs,
    load_sem, row_send, row_recv, col_send, col_recv,
):
    rows, cols, chunks, per, ahead, lag = dims
    part_y, part_z = v.shape[1], v.shape[2]
    grid_x, grid_y = v.shape[0], rbuf.shape[1]
    share_y, grid_z = zbuf.shape[1], zbuf.shape[2]
    tiles, tile = t.shape[1], t.shape[3]
    r, c = lax.axis_index("row"), lax.axis_index("col")

    load_v = pltpu.make_async_copy(v_hbm, v, load_sem.at[0])
    load_w = pltpu.make_async_copy(w_hbm, w, load_sem.at[1])
    load_t = pltpu.make_async_copy(t_hbm, t, load_sem.at[2])
    load_v.start()
    load_w.start()
    load_t.start()

    row_masks = sorted(range(1, rows), key=lambda m: (-bin(m // 2).count("1"), m))
    row_peers = [flipped(r, m) for m in row_masks]
    col_peers = [flipped(c, m) for m in sorted(range(1, cols), reverse=True)]

    barrier = pltpu.get_barrier_semaphore()
    for s in row_peers:
        pl.semaphore_signal(barrier, inc=1, device_id=(s, c), device_id_type=MESH)
    for s in col_peers:
        pl.semaphore_signal(barrier, inc=1, device_id=(r, s), device_id_type=MESH)

    load_v.wait()
    step = SUB * SUB

    def part_loop(i, carry):
        for g in range(part_y // SUB):
            block = v[pl.ds(i * SUB, SUB), g * SUB:(g + 1) * SUB, :].reshape(step, part_z)
            high, low = split(block)
            v_parts[g, 0, pl.ds(pl.multiple_of(i * step, step), step), :] = high
            v_parts[g, 1, pl.ds(pl.multiple_of(i * step, step), step), :] = low
        return carry

    lax.fori_loop(0, grid_x // SUB, part_loop, 0)
    load_w.wait()
    pl.semaphore_wait(barrier, len(row_peers) + len(col_peers))

    def x_stage(k):
        m = w.shape[1] // 2
        for g in range(part_y // SUB):
            both = product(w[k], v_parts[g, 0])
            sums = both[:m] + both[m:] + product(w[k, :m], v_parts[g, 1])
            xs[k, :, g * SUB:(g + 1) * SUB, :] = sums.reshape(rows * per, SUB, part_z)

    def row_stage(k):
        for s in row_peers:
            pltpu.make_async_remote_copy(
                src_ref=xs.at[k, pl.ds(s * per, per)],
                dst_ref=rbuf.at[pl.ds(k * per, per), pl.ds(pl.multiple_of(r * part_y, SUB), part_y), :],
                send_sem=row_send.at[k], recv_sem=row_recv.at[k],
                device_id=(s, c), device_id_type=MESH,
            ).start()
        rbuf[pl.ds(k * per, per), pl.ds(pl.multiple_of(r * part_y, SUB), part_y), :] = xs[k, pl.ds(r * per, per)]

    def row_bytes(k, sem):
        ref = rbuf.at[pl.ds(k * per, per), pl.ds(0, grid_y - part_y), :]
        return pltpu.make_async_copy(ref, ref, sem.at[k])

    def col_bytes(k, sem):
        ref = zbuf.at[pl.ds(k * per, per), :, pl.ds(0, grid_z - part_z)]
        return pltpu.make_async_copy(ref, ref, sem.at[k])

    def y_stage(k):
        row_bytes(k, row_recv).wait()
        for i in range(per):
            high, low = split(rbuf[k * per + i])
            both = product(h_ref[...], high)
            ybuf[k, i] = both[:grid_y] + both[grid_y:] + product(h_ref[:grid_y], low)
        for s in col_peers:
            pltpu.make_async_remote_copy(
                src_ref=ybuf.at[k, :, pl.ds(pl.multiple_of(s * share_y, SUB), share_y), :],
                dst_ref=zbuf.at[pl.ds(k * per, per), :, pl.ds(pl.multiple_of(c * part_z, 128), part_z)],
                send_sem=col_send.at[k], recv_sem=col_recv.at[k],
                device_id=(r, s), device_id_type=MESH,
            ).start()
        zbuf[pl.ds(k * per, per), :, pl.ds(pl.multiple_of(c * part_z, 128), part_z)] = (
            ybuf[k, :, pl.ds(pl.multiple_of(c * share_y, SUB), share_y), :]
        )

    def z_stage(k):
        col_bytes(k, col_recv).wait()
        m = per * share_y
        high, low = split(zbuf[pl.ds(k * per, per)].reshape(m, grid_z))
        lhs[:m] = high
        lhs[m:] = low

        def tile_loop(n, carry):
            both = product(lhs[...], t[0, n])
            sums = both[:m] + both[m:] + product(lhs[:m], t[1, n])
            out_ref[pl.ds(k * per, per), :, pl.ds(pl.multiple_of(n * tile, tile), tile)] = (
                sums.reshape(per, share_y, tile)
            )
            return carry

        lax.fori_loop(0, tiles, tile_loop, 0)

    def loop(k, carry):
        @pl.when(k < chunks)
        def _():
            x_stage(k)
            row_stage(k)

        @pl.when((k >= ahead) & (k < chunks + ahead))
        def _():
            y_stage(k - ahead)

        @pl.when(k == ahead + lag)
        def _():
            load_t.wait()

        @pl.when(k >= ahead + lag)
        def _():
            z_stage(k - ahead - lag)

        return carry

    lax.fori_loop(0, chunks + ahead + lag, loop, 0)

    def drain(k, carry):
        row_bytes(k, row_send).wait()
        col_bytes(k, col_send).wait()
        return carry

    lax.fori_loop(0, chunks, drain, 0)


def transformed(rows, cols, velocity):
    grid_x, part_y, part_z = velocity.shape
    grid_y, grid_z = part_y * rows, part_z * cols
    share_x, share_y = grid_x // rows, grid_y // cols
    chunks = min(8, share_x)
    per = share_x // chunks
    tile = 256
    hx, hy, hz = fixed_table(grid_x), fixed_table(grid_y), fixed_table(grid_z)
    order = np.arange(grid_x).reshape(rows, chunks, per).transpose(1, 0, 2).reshape(chunks, rows * per)
    w = np.stack([np.kron(hx[o], np.eye(SUB, dtype=np.float32)) for o in order])
    w = np.concatenate(halves(w), axis=1)
    h = np.concatenate(halves(hy), axis=0)
    t = np.stack(halves(hz)).reshape(2, grid_z, grid_z // tile, tile).transpose(0, 2, 1, 3)
    f32, bf16 = jnp.float32, jnp.bfloat16
    any_spec = pl.BlockSpec(memory_space=pl.ANY)
    vmem = pl.BlockSpec(memory_space=pltpu.VMEM)
    return pl.pallas_call(
        functools.partial(kernel, (rows, cols, chunks, per, 1, 2)),
        out_shape=jax.ShapeDtypeStruct((share_x, share_y, grid_z), f32),
        in_specs=[any_spec, any_spec, vmem, any_spec],
        out_specs=vmem,
        scratch_shapes=[
            pltpu.VMEM(velocity.shape, f32),
            pltpu.VMEM(w.shape, bf16),
            pltpu.VMEM(t.shape, bf16),
            pltpu.VMEM((part_y // SUB, 2, grid_x * SUB, part_z), bf16),
            pltpu.VMEM((chunks, rows * per, part_y, part_z), f32),
            pltpu.VMEM((share_x, grid_y, part_z), f32),
            pltpu.VMEM((chunks, per, grid_y, part_z), f32),
            pltpu.VMEM((share_x, share_y, grid_z), f32),
            pltpu.VMEM((2 * per * share_y, grid_z), bf16),
            pltpu.SemaphoreType.DMA((3,)),
            pltpu.SemaphoreType.DMA((chunks,)),
            pltpu.SemaphoreType.DMA((chunks,)),
            pltpu.SemaphoreType.DMA((chunks,)),
            pltpu.SemaphoreType.DMA((chunks,)),
        ],
        compiler_params=pltpu.CompilerParams(
            collective_id=0, has_side_effects=True, vmem_limit_bytes=58 * 2**20
        ),
    )(velocity, jnp.asarray(w), jnp.asarray(h), jnp.asarray(np.ascontiguousarray(t)))


def fits(rows, cols, shape):
    grid_x, part_y, part_z = shape
    grid_z = part_z * cols
    held = 7 * grid_x * part_y * part_z * 4 + 4 * grid_z * grid_z + 4 * (grid_x * SUB) ** 2
    even = rows & (rows - 1) == 0 and cols & (cols - 1) == 0 and grid_x % (8 * rows) == 0
    return even and part_y % SUB == 0 and part_z % 128 == 0 and (part_y * rows) % (SUB * cols) == 0 and held < 54 * 2**20


def local(rows, cols, velocity, symbol_x, symbol_y, symbol_z):
    if fits(rows, cols, velocity.shape):
        pencil_values = transformed(rows, cols, velocity)
    else:
        part_values = along_dim(velocity, 0)
        part_values = lax.all_to_all(part_values, "row", split_axis=0, concat_axis=1, tiled=True)
        pencil_values = along_dim(part_values, 1)
        pencil_values = lax.all_to_all(pencil_values, "col", split_axis=1, concat_axis=2, tiled=True)
        pencil_values = along_dim(pencil_values, 2)
    share_x = pencil_values.shape[0]
    part_x = lax.dynamic_slice_in_dim(symbol_x, lax.axis_index("row") * share_x, share_x)
    share_y = pencil_values.shape[1]
    part_y = lax.dynamic_slice_in_dim(symbol_y, lax.axis_index("col") * share_y, share_y)
    symbol = part_x[:, None, None] + part_y[None, :, None] + symbol_z[None, None, :]
    return pencil_values * ((1.0 - 0.2 * symbol) / (1.0 + 0.2 * symbol))


def solution(mesh):
    placed = (P(None, "row", "col"), P(), P(), P())
    return jax.shard_map(
        functools.partial(local, mesh.shape["row"], mesh.shape["col"]),
        mesh=mesh, in_specs=placed, out_specs=P("row", "col", None), check_vma=False,
    )
```

time: 225 us -> 121 us (0.54)
  Pallas kernels: 0 us -> 114 us
  other arithmetic: 67.8 us -> 5.4 us
  blocking collectives: 52.8 us -> 0 us
  matrix products: 51 us -> 0 us
  waiting for transfers between devices: 24.7 us -> 0 us
  local copies, waits for them, and re-layouts: 21.9 us -> 1.46 us
  starting transfers between devices: 5.15 us -> 0 us
    pallas_call x0 -> x1, Pallas kernels: none -> 114 us  [transformed(): pl.pallas_call(functools.partial(kernel, (rows, cols, chunks, per, 1, 2))...]
    dot_general x1 -> x0, other arithmetic: 67.7 us -> none  [along_dim(): jnp.tensordot(values, mode_table(values.shape[dim]), axes=([dim], [0]), p...]
    all_to_all x1 -> x0, blocking collectives: 52.8 us -> none  [local(): lax.all_to_all(part_values, 'row', split_axis=0, concat_axis=1, tiled=True)]
    dot_general x3 -> x0, matrix products: 51 us -> none  [along_dim(): jnp.tensordot(values, mode_table(values.shape[dim]), axes=([dim], [0]), p...]
    all_to_all x1 -> x0, waiting for transfers between devices: 24.7 us -> none  [local(): lax.all_to_all(pencil_values, 'col', split_axis=1, concat_axis=2, tiled=T...]
    all_to_all x3 -> x0, local copies, waits for them, and re-layouts: 13.8 us -> none  [the longest x2 13 us: local(): lax.all_to_all(pencil_values, 'col', split_axis=1, concat_axis=2, tiled=T...]
    transpose x1 -> x0, local copies, waits for them, and re-layouts: 5.51 us -> none  [along_dim(): return jnp.moveaxis(moved, -1, dim)]
    mul x0 -> x1, other arithmetic: none -> 5.32 us  [local(): return pencil_values * ((1.0 - 0.2 * symbol) / (1.0 + 0.2 * symbol))]
  transfers between devices with their start and end apart: 1 -> 0, of which waited for: 1 -> 0; matrix products, arithmetic and copies ran while one was open for 30% -> 0% of each run, Pallas kernels for 0% -> 0%
where the time goes in v1:
time: 121 us
  Pallas kernels  114 us (94%)
  other arithmetic  5.4 us (4%)
  local copies, waits for them, and re-layouts  1.46 us (1%)
    pallas_call x1, Pallas kernels, transformed(): pl.pallas_call(functools.partial(kernel, (rows, cols, chunks, per, 1, 2))...  114 us
    mul x1, other arithmetic, local(): return pencil_values * ((1.0 - 0.2 * symbol) / (1.0 + 0.2 * symbol))  5.32 us

profile of v1, /device:TPU:1, one launch (start us, length us, event | category | flops | bytes accessed | tf_op | source)
XLA Modules:
  0.0 120.7 jit_solution(43900359295177694)
XLA Ops:
  0.0 0.7 dynamic_slice.7
  0.7 0.7 dynamic_slice.6
  1.5 0.1 broadcast_add_fusion
  1.5 0.0 copy-start
  1.5 113.8 %shard_map.73 = f32[16,32,2048]{2,1,0:T(8,128)} custom-call(f32[128,16,512]{2,1,0:T(8,128)} %v_hbm.1, bf16[8,256,1024]{2,1,0:T(8,128)(2,1)} %constant.27.clone.w_hbm, bf16[256,128]{1,0:T(8,128)(2,1)} %constant.28.clone.h_ref, bf16[2,8,2048,256]{3,2,1,0:T(8,128)(2,1)} %constant.29.clone.t_hbm), custom_call_target="tpu_custom_call" | custom-call | tf_op jit(solution)/shard_map/pallas_call | solution.py:209
  115.4 0.0 copy-done
  115.4 5.3 %divide_multiply_fusion = f32[16,32,2048]{2,1,0:T(8,128)} fusion(f32[16,32,2048]{2,1,0:T(8,128)} %shard_map.73, f32[2048]{0:T(1024)S(1)} %copy-done, f32[16,32]{1,0:T(8,128)S(1)} %broadcast_add_fusion), kind=kLoop, calls=%fused_computation | loop fusion | flops 6291456 | bytes 8398848 | tf_op jit(solution)/shard_map/mul | solution.py:258
Async XLA Ops:
  1.5 113.8 %copy-start = (f32[2048]{0:T(1024)S(1)}, f32[2048]{0:T(1024)}, u32[]{:S(2)}) copy-start(f32[2048]{0:T(1024)} %param.10) | copy-start | bytes 24580

commit v2 on v1

v2 whole, which is shorter than its diff:
```python
import functools

import jax
import jax.numpy as jnp
import numpy as np
from jax import lax
from jax.experimental import pallas as pl
from jax.experimental.pallas import tpu as pltpu
from jax.sharding import PartitionSpec as P

SUB = 8
MESH = pl.DeviceIdType.MESH


def mode_table(count):
    rank = jnp.arange(count)
    angle = 2.0 * jnp.pi / count * (rank[:, None] * rank[None, :] % count).astype(jnp.float32)
    return (jnp.cos(angle) + jnp.sin(angle)) * count ** (-0.5)


def along_dim(values, dim):
    moved = jnp.tensordot(
        values, mode_table(values.shape[dim]), axes=([dim], [0]), precision=lax.Precision.HIGHEST
    )
    return jnp.moveaxis(moved, -1, dim)


def fixed_table(count):
    rank = np.arange(count)
    angle = 2.0 * np.pi / count * (rank[:, None] * rank[None, :] % count)
    return ((np.cos(angle) + np.sin(angle)) * count ** (-0.5)).astype(np.float32)


def halves(table):
    high = table.astype(jnp.bfloat16)
    low = (table - high.astype(np.float32)).astype(jnp.bfloat16)
    return high, low


def split(values):
    high = values.astype(jnp.bfloat16)
    low = (values - high.astype(jnp.float32)).astype(jnp.bfloat16)
    return high, low


def product(a, b):
    return jnp.dot(a, b, preferred_element_type=jnp.float32)


def flipped(index, mask):
    out = index
    bit = 1
    while bit <= mask:
        if mask & bit:
            out = out + bit * (1 - 2 * ((index // bit) % 2))
        bit *= 2
    return out


def kernel(
    dims, v_hbm, w_hbm, t_hbm, sx_ref, sy_ref, sz_ref, out_ref,
    v, w, t, v_parts, xs, rbuf, ybuf, zbuf, lhs, sx_col, sy_col,
    load_sem, row_send, row_recv, col_send, col_recv,
):
    rows, cols, chunks, per, ahead, lag = dims
    part_y, part_z = v.shape[1], v.shape[2]
    grid_x, grid_y = v.shape[0], rbuf.shape[1]
    share_y, grid_z = zbuf.shape[1], zbuf.shape[2]
    tiles, tile = t.shape[1], t.shape[3]
    r, c = lax.axis_index("row"), lax.axis_index("col")

    load_v = pltpu.make_async_copy(v_hbm, v, load_sem.at[0])
    load_w = pltpu.make_async_copy(w_hbm.at[0], w.at[0], load_sem.at[1])
    load_rest = pltpu.make_async_copy(w_hbm.at[pl.ds(1, chunks - 1)], w.at[pl.ds(1, chunks - 1)], load_sem.at[2])
    load_t = pltpu.make_async_copy(t_hbm, t, load_sem.at[3])
    load_v.start()
    load_w.start()

    row_masks = sorted(range(1, rows), key=lambda m: (-bin(m // 2).count("1"), m))
    row_peers = [flipped(r, m) for m in row_masks]
    col_peers = [flipped(c, m) for m in range(1, cols)]

    barrier = pltpu.get_barrier_semaphore()
    for s in row_peers:
        pl.semaphore_signal(barrier, inc=1, device_id=(s, c), device_id_type=MESH)
    for s in col_peers:
        pl.semaphore_signal(barrier, inc=1, device_id=(r, s), device_id_type=MESH)

    for ref, column in ((sx_ref, sx_col), (sy_ref, sy_col)):
        column[...] = jnp.broadcast_to(ref[...], (128, ref.shape[1])).T
    load_v.wait()
    load_w.wait()
    load_rest.start()
    step = SUB * SUB

    def part_loop(i, carry):
        for g in range(part_y // SUB):
            block = v[pl.ds(i * SUB, SUB), g * SUB:(g + 1) * SUB, :].reshape(step, part_z)
            high, low = split(block)
            v_parts[g, 0, pl.ds(pl.multiple_of(i * step, step), step), :] = high
            v_parts[g, 1, pl.ds(pl.multiple_of(i * step, step), step), :] = low
        return carry

    lax.fori_loop(0, grid_x // SUB, part_loop, 0)
    load_t.start()
    pl.semaphore_wait(barrier, len(row_peers) + len(col_peers))

    def x_stage(k):
        m, depth = rows * per * SUB, grid_x * SUB
        for g in range(part_y // SUB):
            both = product(w[k, :2 * m, :depth], v_parts[g, 0])
            sums = both[:m] + both[m:] + product(w[k, :m, :depth], v_parts[g, 1])
            xs[k, :, g * SUB:(g + 1) * SUB, :] = sums.reshape(rows * per, SUB, part_z)

    def own_rows():
        return pl.ds(pl.multiple_of(r * part_y, SUB), part_y)

    def row_stage(k):
        for i in range(per):
            for s in row_peers:
                pltpu.make_async_remote_copy(
                    src_ref=xs.at[k, s * per + i],
                    dst_ref=rbuf.at[k * per + i, own_rows(), :],
                    send_sem=row_send.at[k], recv_sem=row_recv.at[k, i],
                    device_id=(s, c), device_id_type=MESH,
                ).start()
        rbuf[pl.ds(k * per, per), own_rows(), :] = xs[k, pl.ds(r * per, per)]

    def y_stage(k):
        for i in range(per):
            came = rbuf.at[k * per + i, pl.ds(0, grid_y - part_y), :]
            pltpu.make_async_copy(came, came, row_recv.at[k, i]).wait()
            high, low = split(rbuf[k * per + i])
            both = product(w[0, :2 * grid_y, grid_x * SUB:], high)
            ybuf[k, i] = both[:grid_y] + both[grid_y:] + product(w[0, :grid_y, grid_x * SUB:], low)
            for m, s in enumerate(col_peers):
                pltpu.make_async_remote_copy(
                    src_ref=ybuf.at[k, i, pl.ds(pl.multiple_of(s * share_y, SUB), share_y), :],
                    dst_ref=zbuf.at[k * per + i, :, pl.ds(pl.multiple_of(c * part_z, 128), part_z)],
                    send_sem=col_send.at[k], recv_sem=col_recv.at[k, m],
                    device_id=(r, s), device_id_type=MESH,
                ).start()
        zbuf[pl.ds(k * per, per), :, pl.ds(pl.multiple_of(c * part_z, 128), part_z)] = (
            ybuf[k, :, pl.ds(pl.multiple_of(c * share_y, SUB), share_y), :]
        )

    def col_wait(k, m):
        came = zbuf.at[pl.ds(k * per, per), :, pl.ds(0, part_z)]
        pltpu.make_async_copy(came, came, col_recv.at[k, m]).wait()

    def scaled(k, n, sums):
        y_part = sy_col[pl.ds(pl.multiple_of(c * share_y, SUB), share_y), :]
        z_part = sz_ref[:, pl.ds(pl.multiple_of(n * tile, tile), tile)]
        plane = jnp.concatenate([y_part] * (tile // 128), axis=1) + z_part
        for i in range(per):
            x_part = sx_col[pl.ds(r * chunks * per + k * per + i, 1), :]
            symbol = jnp.concatenate([x_part] * (tile // 128), axis=1) + plane
            factor = (1.0 - 0.2 * symbol) / (1.0 + 0.2 * symbol)
            out_ref[k * per + i, :, pl.ds(pl.multiple_of(n * tile, tile), tile)] = (
                sums[i * share_y:(i + 1) * share_y] * factor
            )

    size = per * share_y

    def z_stage(k):
        for m in range(len(col_peers)):
            col_wait(k, m)
        high, low = split(zbuf[pl.ds(k * per, per)].reshape(size, grid_z))
        lhs[:size] = high
        lhs[size:] = low

        def tile_loop(n, carry):
            both = product(lhs[...], t[0, n])
            scaled(k, n, both[:size] + both[size:] + product(lhs[:size], t[1, n]))
            return carry

        lax.fori_loop(0, tiles, tile_loop, 0)

    def last_z_stage(k):
        for m, s in enumerate([c] + col_peers):
            if m > 0:
                col_wait(k, m - 1)
            span = pl.ds(pl.multiple_of(s * part_z, 128), part_z)
            high, low = split(zbuf[pl.ds(k * per, per), :, span].reshape(size, part_z))
            lhs[:size, :part_z] = high
            lhs[size:, :part_z] = low

            def tile_loop(n, carry):
                both = product(lhs[:, :part_z], t[0, n, span, :])
                sums = both[:size] + both[size:] + product(lhs[:size, :part_z], t[1, n, span, :])
                at = pl.ds(pl.multiple_of(n * tile, tile), tile)
                if m > 0:
                    sums = sums + out_ref[pl.ds(k * per, per), :, at].reshape(size, tile)
                if m < len(col_peers):
                    out_ref[pl.ds(k * per, per), :, at] = sums.reshape(per, share_y, tile)
                else:
                    scaled(k, n, sums)
                return carry

            lax.fori_loop(0, tiles, tile_loop, 0)

    def loop(k, carry):
        @pl.when(k == 1)
        def _():
            load_rest.wait()

        @pl.when(k < chunks)
        def _():
            x_stage(k)
            row_stage(k)

        @pl.when((k >= ahead) & (k < chunks + ahead))
        def _():
            y_stage(k - ahead)

        @pl.when(k == ahead + lag)
        def _():
            load_t.wait()

        @pl.when(k >= ahead + lag)
        def _():
            z_stage(k - ahead - lag)

        return carry

    lax.fori_loop(0, chunks + ahead + lag - 1, loop, 0)
    last_z_stage(chunks - 1)

    def drain(k, carry):
        sent = rbuf.at[pl.ds(k * per, per), pl.ds(0, grid_y - part_y), :]
        pltpu.make_async_copy(sent, sent, row_send.at[k]).wait()
        sent = zbuf.at[pl.ds(k * per, per), :, pl.ds(0, grid_z - part_z)]
        pltpu.make_async_copy(sent, sent, col_send.at[k]).wait()
        return carry

    lax.fori_loop(0, chunks, drain, 0)


def transformed(rows, cols, velocity, symbol_x, symbol_y, symbol_z):
    grid_x, part_y, part_z = velocity.shape
    grid_y, grid_z = part_y * rows, part_z * cols
    share_x, share_y = grid_x // rows, grid_y // cols
    chunks = min(8, share_x)
    per = share_x // chunks
    tile = 256
    hx, hy, hz = fixed_table(grid_x), fixed_table(grid_y), fixed_table(grid_z)
    order = np.arange(grid_x).reshape(rows, chunks, per).transpose(1, 0, 2).reshape(chunks, rows * per)
    w = np.stack([np.kron(hx[o], np.eye(SUB, dtype=np.float32)) for o in order])
    w = np.concatenate(halves(w), axis=1)
    h = np.concatenate(halves(hy), axis=0)
    t = np.stack(halves(hz)).reshape(2, grid_z, grid_z // tile, tile).transpose(0, 2, 1, 3)
    held = np.zeros((chunks, max(w.shape[1], h.shape[0]), w.shape[2] + h.shape[1]), w.dtype)
    held[:, :w.shape[1], :w.shape[2]] = w
    held[0, :h.shape[0], w.shape[2]:] = h
    f32, bf16 = jnp.float32, jnp.bfloat16
    hbm = pl.BlockSpec(memory_space=pltpu.HBM)
    vmem = pl.BlockSpec(memory_space=pltpu.VMEM)
    return pl.pallas_call(
        functools.partial(kernel, (rows, cols, chunks, per, 1, 2)),
        out_shape=jax.ShapeDtypeStruct((share_x, share_y, grid_z), f32),
        in_specs=[hbm, hbm, hbm, vmem, vmem, vmem],
        out_specs=vmem,
        scratch_shapes=[
            pltpu.VMEM(velocity.shape, f32),
            pltpu.VMEM(held.shape, bf16),
            pltpu.VMEM(t.shape, bf16),
            pltpu.VMEM((part_y // SUB, 2, grid_x * SUB, part_z), bf16),
            pltpu.VMEM((chunks, rows * per, part_y, part_z), f32),
            pltpu.VMEM((share_x, grid_y, part_z), f32),
            pltpu.VMEM((chunks, per, grid_y, part_z), f32),
            pltpu.VMEM((share_x, share_y, grid_z), f32),
            pltpu.VMEM((2 * per * share_y, grid_z), bf16),
            pltpu.VMEM((grid_x, 128), f32),
            pltpu.VMEM((grid_y, 128), f32),
            pltpu.SemaphoreType.DMA((4,)),
            pltpu.SemaphoreType.DMA((chunks,)),
            pltpu.SemaphoreType.DMA((chunks, per)),
            pltpu.SemaphoreType.DMA((chunks,)),
            pltpu.SemaphoreType.DMA((chunks, cols - 1)),
        ],
        compiler_params=pltpu.CompilerParams(
            collective_id=0, has_side_effects=True, vmem_limit_bytes=46 * 2**20
        ),
    )(velocity, jnp.asarray(held), jnp.asarray(np.ascontiguousarray(t)),
      symbol_x[None, :], symbol_y[None, :], symbol_z[None, :])


def fits(rows, cols, shape):
    grid_x, part_y, part_z = shape
    grid_z = part_z * cols
    held = 7 * grid_x * part_y * part_z * 4 + 4 * grid_z * grid_z + 4 * (grid_x * SUB) ** 2
    even = rows & (rows - 1) == 0 and cols & (cols - 1) == 0 and grid_x % (8 * rows) == 0
    return even and part_y % SUB == 0 and part_z % 128 == 0 and (part_y * rows) % (SUB * cols) == 0 and held < 54 * 2**20


def local(rows, cols, velocity, symbol_x, symbol_y, symbol_z):
    if fits(rows, cols, velocity.shape):
        return transformed(rows, cols, velocity, symbol_x, symbol_y, symbol_z)
    part_values = along_dim(velocity, 0)
    part_values = lax.all_to_all(part_values, "row", split_axis=0, concat_axis=1, tiled=True)
    pencil_values = along_dim(part_values, 1)
    pencil_values = lax.all_to_all(pencil_values, "col", split_axis=1, concat_axis=2, tiled=True)
    pencil_values = along_dim(pencil_values, 2)
    share_x = pencil_values.shape[0]
    part_x = lax.dynamic_slice_in_dim(symbol_x, lax.axis_index("row") * share_x, share_x)
    share_y = pencil_values.shape[1]
    part_y = lax.dynamic_slice_in_dim(symbol_y, lax.axis_index("col") * share_y, share_y)
    symbol = part_x[:, None, None] + part_y[None, :, None] + symbol_z[None, None, :]
    return pencil_values * ((1.0 - 0.2 * symbol) / (1.0 + 0.2 * symbol))


def solution(mesh):
    placed = (P(None, "row", "col"), P(), P(), P())
    return jax.shard_map(
        functools.partial(local, mesh.shape["row"], mesh.shape["col"]),
        mesh=mesh, in_specs=placed, out_specs=P("row", "col", None), check_vma=False,
    )
```

time: 121 us -> 113 us (0.934)
  other arithmetic: 5.4 us -> 0 us
  Pallas kernels: 114 us -> 109 us
  local copies, waits for them, and re-layouts: 1.46 us -> 4.02 us
    mul x1 -> x0, other arithmetic: 5.32 us -> none  [local(): return pencil_values * ((1.0 - 0.2 * symbol) / (1.0 + 0.2 * symbol))]
    pallas_call x1, Pallas kernels: 114 us -> 109 us  [transformed(): pl.pallas_call(functools.partial(kernel, (rows, cols, chunks, per, 1, 2))...]
    unnamed x2 -> x7, local copies, waits for them, and re-layouts: 0.01 us -> 4.02 us
    dynamic_slice x2 -> x0, local copies, waits for them, and re-layouts: 1.45 us -> none  [the longest x1 0.73 us: local(): lax.dynamic_slice_in_dim(symbol_y, lax.axis_index('col') * share_y, share_y)]
where the time goes in v2:
time: 113 us
  Pallas kernels  109 us (96%)
  local copies, waits for them, and re-layouts  4.02 us (4%)
    pallas_call x1, Pallas kernels, transformed(): pl.pallas_call(functools.partial(kernel, (rows, cols, chunks, per, 1, 2))...  109 us
    unnamed x7, local copies, waits for them, and re-layouts  4.02 us

profile of v2, /device:TPU:1, one launch (start us, length us, event | category | flops | bytes accessed | tf_op | source)
XLA Modules:
  0.0 113.3 jit_solution(5034621838582773465)
XLA Ops:
  0.0 0.0 copy-start
  0.0 0.7 copy-done
  0.7 0.0 copy-start.1
  0.7 0.7 copy-done.1
  1.4 0.0 copy-start.2
  1.4 0.7 copy-done.2
  2.0 109.2 %shard_map.64 = f32[16,32,2048]{2,1,0:T(8,128)S(1)} custom-call(f32[128,16,512]{2,1,0:T(8,128)} %v_hbm.1, bf16[8,256,1152]{2,1,0:T(8,128)(2,1)} %constant.4.clone.w_hbm, bf16[2,8,2048,256]{3,2,1,0:T(8,128)(2,1)} %constant.5.clone.t_hbm, f32[1,128]{1,0:T(1,128)S(1)} %bitcast.4, f32[1,128]{1,0:T(1,128)S(1)} %bitcast.5, f32[1,2048]{1,0:T(1,128)S(1)} %bitcast.3), custom_call_target="tpu_custom_call" | custom-call | tf_op jit(solution)/shard_map/pallas_call | solution.py:258
  111.2 2.0 %copy.8 = f32[16,32,2048]{2,1,0:T(8,128)} copy(f32[16,32,2048]{2,1,0:T(8,128)S(1)} %shard_map.64) | data formatting | bytes 8388608
Async XLA Ops:
  0.0 0.7 copy-start
  0.7 0.7 copy-start.1
  1.4 0.7 copy-start.2

commit v3 on v2

--- a/solution.py
+++ b/solution.py
@@ -69,11 +69,19 @@
     tiles, tile = t.shape[1], t.shape[3]
     r, c = lax.axis_index("row"), lax.axis_index("col")
 
-    load_v = pltpu.make_async_copy(v_hbm, v, load_sem.at[0])
+    pieces = 4 if grid_x % (4 * SUB) == 0 else 1
+    piece = grid_x // pieces
+    load_v = [
+        pltpu.make_async_copy(
+            v_hbm.at[pl.ds(p * piece, piece)], v.at[pl.ds(p * piece, piece)], load_sem.at[3 + p]
+        )
+        for p in range(pieces)
+    ]
     load_w = pltpu.make_async_copy(w_hbm.at[0], w.at[0], load_sem.at[1])
     load_rest = pltpu.make_async_copy(w_hbm.at[pl.ds(1, chunks - 1)], w.at[pl.ds(1, chunks - 1)], load_sem.at[2])
-    load_t = pltpu.make_async_copy(t_hbm, t, load_sem.at[3])
-    load_v.start()
+    load_t = pltpu.make_async_copy(t_hbm, t, load_sem.at[0])
+    for load in load_v:
+        load.start()
     load_w.start()
 
     row_masks = sorted(range(1, rows), key=lambda m: (-bin(m // 2).count("1"), m))
@@ -88,9 +96,6 @@
 
     for ref, column in ((sx_ref, sx_col), (sy_ref, sy_col)):
         column[...] = jnp.broadcast_to(ref[...], (128, ref.shape[1])).T
-    load_v.wait()
-    load_w.wait()
-    load_rest.start()
     step = SUB * SUB
 
     def part_loop(i, carry):
@@ -101,7 +106,11 @@
             v_parts[g, 1, pl.ds(pl.multiple_of(i * step, step), step), :] = low
         return carry
 
-    lax.fori_loop(0, grid_x // SUB, part_loop, 0)
+    for p in range(pieces):
+        load_v[p].wait()
+        lax.fori_loop(p * piece // SUB, (p + 1) * piece // SUB, part_loop, 0)
+    load_w.wait()
+    load_rest.start()
     load_t.start()
     pl.semaphore_wait(barrier, len(row_peers) + len(col_peers))
 
@@ -272,7 +281,7 @@
             pltpu.VMEM((2 * per * share_y, grid_z), bf16),
             pltpu.VMEM((grid_x, 128), f32),
             pltpu.VMEM((grid_y, 128), f32),
-            pltpu.SemaphoreType.DMA((4,)),
+            pltpu.SemaphoreType.DMA((7,)),
             pltpu.SemaphoreType.DMA((chunks,)),
             pltpu.SemaphoreType.DMA((chunks, per)),
             pltpu.SemaphoreType.DMA((chunks,)),

time: 113 us -> 113 us (level)
  no operation moved by 1% of the time
where the time goes in v3:
time: 113 us
  Pallas kernels  109 us (96%)
  local copies, waits for them, and re-layouts  4.02 us (4%)
    pallas_call x1, Pallas kernels, transformed(): pl.pallas_call(functools.partial(kernel, (rows, cols, chunks, per, 1, 2))...  109 us
    unnamed x7, local copies, waits for them, and re-layouts  4.02 us

profile of v3, /device:TPU:1, one launch (start us, length us, event | category | flops | bytes accessed | tf_op | source)
XLA Modules:
  0.0 112.7 jit_solution(15758148026286314814)
XLA Ops:
  0.0 0.0 copy-start
  0.0 0.7 copy-done
  0.7 0.0 copy-start.1
  0.7 0.7 copy-done.1
  1.4 0.0 copy-start.2
  1.4 0.7 copy-done.2
  2.0 108.7 %shard_map.64 = f32[16,32,2048]{2,1,0:T(8,128)S(1)} custom-call(f32[128,16,512]{2,1,0:T(8,128)} %v_hbm.1, bf16[8,256,1152]{2,1,0:T(8,128)(2,1)} %constant.4.clone.w_hbm, bf16[2,8,2048,256]{3,2,1,0:T(8,128)(2,1)} %constant.5.clone.t_hbm, f32[1,128]{1,0:T(1,128)S(1)} %bitcast.4, f32[1,128]{1,0:T(1,128)S(1)} %bitcast.5, f32[1,2048]{1,0:T(1,128)S(1)} %bitcast.3), custom_call_target="tpu_custom_call" | custom-call | tf_op jit(solution)/shard_map/pallas_call | solution.py:267
  110.7 2.0 %copy.8 = f32[16,32,2048]{2,1,0:T(8,128)} copy(f32[16,32,2048]{2,1,0:T(8,128)S(1)} %shard_map.64) | data formatting | bytes 8388608
Async XLA Ops:
  0.0 0.7 copy-start
  0.7 0.7 copy-start.1
  1.4 0.7 copy-start.2
